TPU v7x, 32 devices: a whole 2x2x4 slice. The times are simulated.
32 devices in a mesh: section: 8 (over y, x, core), expert: 4 (over z).
Axes of the slice: x: 2, y: 2, z: 4, core: 2. Of those that a mesh axis runs over, the one named last changes fastest.
Arguments:
- top_grad: bfloat16 [2, 64, 2048], P(None, 'expert'), may hold values from -6 to 6
- layer_input: bfloat16 [8, 2, 64, 2048], P('section', None, 'expert'), may hold values from -6 to 6
- expert_out: bfloat16 [8, 2, 64, 2, 2048], P('section', None, 'expert'), may hold values from -3 to 3
- router_w: float32 [8, 2048, 8], P('section'), may hold values from -0.375 to 0.375
- expert_ids: int32 [8, 2, 64, 2], P('section', None, 'expert'), may hold values from 0 to 7, as said below
- hidden: bfloat16 [8, 2, 32, 7168], P('section', None, None, 'expert'), may hold values from -0.59765625 to 0.59765625
- down_w: bfloat16 [8, 7168, 2048], P('section', 'expert'), may hold values from -0.0625 to 0.0625
Outputs:
- input_grad: bfloat16 [8, 2, 64, 2048], P('section', None, 'expert')
- router_grad: float32 [8, 2048, 8], P('section')
- hidden_grad: bfloat16 [8, 2, 32, 7168], P('section', None, None, 'expert')
- down_grad: bfloat16 [8, 7168, 2048], P('section', 'expert')
Inputs may be any that keep to these rules, and one draw needn't show every extreme that they name: `expert_ids`: the two experts of a token differ. In each micro-batch, the 16 tokens of one device choose expert 0 at most 8 times, and exactly 8 times in some blocks of every draw.
All inputs are finite; a program needn't handle non-finite values.
Results may differ from a plain program's by a relative error of at most 0.024.
Values may be sent and summed in bfloat16 or wider, within the bound.
A program may use at most 64 MiB of HBM per device.

v0:
```python
import jax
import jax.numpy as jnp
from jax import lax
from jax.sharding import PartitionSpec as P


def passed_along(value, axis, by):
    count = lax.axis_size(axis)
    pairs = [(i, i + by) for i in range(count) if 0 <= i + by < count]
    return lax.ppermute(value, axis, pairs)


def gate_pair(inputs, weights, chosen):
    logits = jnp.einsum(
        "mtd,de->mte", inputs.astype(jnp.float32), weights, precision=lax.Precision.HIGHEST
    )
    select = (chosen[..., None] == jnp.arange(weights.shape[1], dtype=jnp.int32)).astype(
        jnp.float32
    )
    picked = jnp.sum(select * logits[..., None, :], axis=-1)
    gate_first = jax.nn.sigmoid(picked[..., 0] - picked[..., 1])
    return (gate_first, select)


def backprop(cotangent, inputs, outputs, weights, select, gate_first):
    cot_float = cotangent.astype(jnp.float32)
    gate_dot = jnp.einsum("mtkd,mtd->mtk", outputs, cotangent, preferred_element_type=jnp.float32)
    logit_diff = gate_first * (1.0 - gate_first) * (gate_dot[..., 0] - gate_dot[..., 1])
    logit_grad = logit_diff[..., None] * (select[..., 0, :] - select[..., 1, :])
    passed = cot_float + jnp.einsum(
        "mte,de->mtd", logit_grad, weights, precision=lax.Precision.HIGHEST
    )
    router_part = jnp.einsum(
        "mtd,mte->de", inputs.astype(jnp.float32), logit_grad, precision=lax.Precision.HIGHEST
    )
    return (passed.astype(jnp.bfloat16), router_part)


def dispatch_rows(cotangent, gate_first, chosen, capacity):
    is_zero = (chosen == 0).astype(jnp.float32)
    zero_gate = gate_first * is_zero[..., 0] + (1.0 - gate_first) * is_zero[..., 1]
    routed = is_zero[..., 0] + is_zero[..., 1]
    slot_pos = (jnp.cumsum(routed, axis=-1) - routed).astype(jnp.int32)
    slot_ids = jnp.arange(capacity, dtype=jnp.int32)
    pick_table = (
        (slot_pos[..., None, :] == slot_ids[:, None]) & (routed[..., None, :] > 0.5)
    ).astype(jnp.float32)
    scaled = zero_gate[..., None] * cotangent.astype(jnp.float32)
    rows_out = jnp.einsum("mbcu,mbud->mbcd", pick_table, scaled, precision=lax.Precision.HIGHEST)
    return rows_out.astype(jnp.bfloat16)


def per_device(top_grad, layer_input, expert_out, router_w, expert_ids, hidden, down_w):
    section_count = lax.axis_size("section")
    section_index = lax.axis_index("section")
    micro_count = top_grad.shape[0]
    tok_rows = top_grad.shape[1]
    width = top_grad.shape[2]
    inputs = layer_input[0]
    saved_outs = expert_out[0]
    router = router_w[0]
    chosen = expert_ids[0]
    gate_first, select = gate_pair(inputs, router, chosen)
    is_last = section_index == section_count - 1
    empty_cot = jnp.zeros((micro_count, tok_rows, width), jnp.bfloat16)
    empty_router = jnp.zeros((width, router.shape[1]), jnp.float32)

    def advance_all(moment, totals):
        arrived, section_dy, section_dx, router_acc = totals
        active = moment == section_count - 1 - section_index
        cotangent = jnp.where(is_last, top_grad, arrived)
        passed, router_part = backprop(cotangent, inputs, saved_outs, router, select, gate_first)
        section_dy = jnp.where(active, cotangent, section_dy)
        section_dx = jnp.where(active, passed, section_dx)
        router_acc = router_acc + jnp.where(active, router_part, 0.0)
        arrived = passed_along(passed, "section", -1)
        return (arrived, section_dy, section_dx, router_acc)

    start_state = (empty_cot, empty_cot, empty_cot, empty_router)
    _, section_dy, section_dx, router_acc = lax.fori_loop(
        0, section_count, advance_all, start_state
    )
    total_tokens = micro_count * tok_rows * lax.axis_size("expert")
    router_grad = lax.psum(router_acc, "expert") / total_tokens
    capacity = tok_rows // 2
    rows_out = dispatch_rows(section_dy[:, None], gate_first[:, None], chosen[:, None], capacity)
    rows_out = rows_out.reshape(micro_count, capacity, width)
    saved_hidden = hidden[0]
    weight = down_w[0]
    ff_local = weight.shape[0]
    slot_total = saved_hidden.shape[1]
    gathered = lax.all_gather(rows_out, "expert", axis=1, tiled=True)
    flat_rows = gathered.reshape(-1, width)
    hidden_acc = lax.dot_general(
        flat_rows, weight, (((1,), (1,)), ((), ())), preferred_element_type=jnp.float32
    )
    hidden_acc = hidden_acc.astype(jnp.bfloat16).reshape(micro_count, slot_total, ff_local)
    weight_sum = lax.dot_general(
        saved_hidden.reshape(-1, ff_local),
        flat_rows,
        (((0,), (0,)), ((), ())),
        preferred_element_type=jnp.float32,
    )
    return (
        section_dx[None],
        router_grad[None],
        hidden_acc[None],
        weight_sum.astype(jnp.bfloat16)[None],
    )


def solution(mesh):
    placed = (
        P(None, "expert", None),
        P("section", None, "expert", None),
        P("section", None, "expert", None, None),
        P("section", None, None),
        P("section", None, "expert", None),
        P("section", None, None, "expert"),
        P("section", "expert", None),
    )
    return jax.shard_map(
        per_device,
        mesh=mesh,
        in_specs=placed,
        out_specs=(
            P("section", None, "expert", None),
            P("section", None, None),
            P("section", None, None, "expert"),
            P("section", "expert", None),
        ),
        check_vma=False,
    )
```

profile of v0, /device:TPU:0, one launch (start us, length us, event | category | flops | bytes accessed | tf_op | source)
XLA Modules:
  0.0 136.3 jit_solution(297032122991663004)
XLA Ops:
  8.0 1.5 %fusion.22 = f32[2,16,8]{1,2,0:T(8,128)S(1)} fusion(f32[1,2048,8]{1,2,0:T(8,128)} %param.12, bf16[1,2,16,2048]{3,2,1,0:T(8,128)(2,1)} %param.10), kind=kOutput, calls=%fused_computation.29 | convolution fusion | flops 6291456 | bytes 197632 | tf_op jit(solution)/shard_map/mtd,de->mte/dot_general | solution.py:14
  9.5 73.4 %while.22 = (s32[]{:T(128)}, bf16[2,16,2048]{2,1,0:T(8,128)(2,1)S(1)}, bf16[2,16,2048]{2,1,0:T(8,128)(2,1)S(1)}, bf16[2,16,2048]{2,1,0:T(8,128)(2,1)S(1)}, f32[2...) while((s32[]{:T(128)}, ...), condition=%wide.region_2.3_spmd.clone, body=%wide.region_1.2_spmd.clone.sunk | while | flops 13419140 | bytes 2428622 | solution.py:80
  9.7 1.6 %fusion.53 = f32[2,16,1,2]{3,2,1,0:T(1,128)S(1)} fusion(bf16[2,16,2,2048]{3,2,1,0:T(2,128)(2,1)} %get-tuple-element.510, bf16[2,16,2048,1]{2,1,0,3:T(8,128)(2,1)S(1)} %bitcast.83), kind=kOutput, calls=%fused_computation.6.clone.1 | convolution fusion | flops 262144 | bytes 393472 | tf_op jit(solution)/shard_map/while/body/eval_jaxpr/mtkd,mtd->mtk/dot_general | solution.py:27
  12.6 1.3 collective-permute-start
  15.9 1.6 %fusion.53 = f32[2,16,1,2]{3,2,1,0:T(1,128)S(1)} fusion(bf16[2,16,2,2048]{3,2,1,0:T(2,128)(2,1)} %get-tuple-element.510, bf16[2,16,2048,1]{2,1,0,3:T(8,128)(2,1)S(1)} %bitcast.83), kind=kOutput, calls=%fused_computation.6.clone.1 | convolution fusion | flops 262144 | bytes 393472 | tf_op jit(solution)/shard_map/while/body/eval_jaxpr/mtkd,mtd->mtk/dot_general | solution.py:27
  21.4 4.7 %collective-permute-done = bf16[2,16,2048]{2,1,0:T(8,128)(2,1)S(1)} collective-permute-done((bf16[2,16,2048]{2,1,0:T(8,128)(2,1)S(1)}, bf16[2,16,2048]{2,1,0:T(8,128)(2,1)S(1)}, u32[]{:S(2)}, u32[]{:S(2)}) %collective-permute-start) | collective-permute-done | bytes 131104 | tf_op jit(solution)/shard_map/while/body/eval_jaxpr/ppermute | solution.py:10
  26.1 1.6 %fusion.53 = f32[2,16,1,2]{3,2,1,0:T(1,128)S(1)} fusion(bf16[2,16,2,2048]{3,2,1,0:T(2,128)(2,1)} %get-tuple-element.510, bf16[2,16,2048,1]{2,1,0,3:T(8,128)(2,1)S(1)} %bitcast.83), kind=kOutput, calls=%fused_computation.6.clone.1 | convolution fusion | flops 262144 | bytes 393472 | tf_op jit(solution)/shard_map/while/body/eval_jaxpr/mtkd,mtd->mtk/dot_general | solution.py:27
  31.6 3.8 %collective-permute-done = bf16[2,16,2048]{2,1,0:T(8,128)(2,1)S(1)} collective-permute-done((bf16[2,16,2048]{2,1,0:T(8,128)(2,1)S(1)}, bf16[2,16,2048]{2,1,0:T(8,128)(2,1)S(1)}, u32[]{:S(2)}, u32[]{:S(2)}) %collective-permute-start) | collective-permute-done | bytes 131104 | tf_op jit(solution)/shard_map/while/body/eval_jaxpr/ppermute | solution.py:10
  35.5 1.6 %fusion.53 = f32[2,16,1,2]{3,2,1,0:T(1,128)S(1)} fusion(bf16[2,16,2,2048]{3,2,1,0:T(2,128)(2,1)} %get-tuple-element.510, bf16[2,16,2048,1]{2,1,0,3:T(8,128)(2,1)S(1)} %bitcast.83), kind=kOutput, calls=%fused_computation.6.clone.1 | convolution fusion | flops 262144 | bytes 393472 | tf_op jit(solution)/shard_map/while/body/eval_jaxpr/mtkd,mtd->mtk/dot_general | solution.py:27
  40.9 3.8 %collective-permute-done = bf16[2,16,2048]{2,1,0:T(8,128)(2,1)S(1)} collective-permute-done((bf16[2,16,2048]{2,1,0:T(8,128)(2,1)S(1)}, bf16[2,16,2048]{2,1,0:T(8,128)(2,1)S(1)}, u32[]{:S(2)}, u32[]{:S(2)}) %collective-permute-start) | collective-permute-done | bytes 131104 | tf_op jit(solution)/shard_map/while/body/eval_jaxpr/ppermute | solution.py:10
  44.8 1.6 %fusion.53 = f32[2,16,1,2]{3,2,1,0:T(1,128)S(1)} fusion(bf16[2,16,2,2048]{3,2,1,0:T(2,128)(2,1)} %get-tuple-element.510, bf16[2,16,2048,1]{2,1,0,3:T(8,128)(2,1)S(1)} %bitcast.83), kind=kOutput, calls=%fused_computation.6.clone.1 | convolution fusion | flops 262144 | bytes 393472 | tf_op jit(solution)/shard_map/while/body/eval_jaxpr/mtkd,mtd->mtk/dot_general | solution.py:27
  50.3 3.8 %collective-permute-done = bf16[2,16,2048]{2,1,0:T(8,128)(2,1)S(1)} collective-permute-done((bf16[2,16,2048]{2,1,0:T(8,128)(2,1)S(1)}, bf16[2,16,2048]{2,1,0:T(8,128)(2,1)S(1)}, u32[]{:S(2)}, u32[]{:S(2)}) %collective-permute-start) | collective-permute-done | bytes 131104 | tf_op jit(solution)/shard_map/while/body/eval_jaxpr/ppermute | solution.py:10
  54.2 1.6 %fusion.53 = f32[2,16,1,2]{3,2,1,0:T(1,128)S(1)} fusion(bf16[2,16,2,2048]{3,2,1,0:T(2,128)(2,1)} %get-tuple-element.510, bf16[2,16,2048,1]{2,1,0,3:T(8,128)(2,1)S(1)} %bitcast.83), kind=kOutput, calls=%fused_computation.6.clone.1 | convolution fusion | flops 262144 | bytes 393472 | tf_op jit(solution)/shard_map/while/body/eval_jaxpr/mtkd,mtd->mtk/dot_general | solution.py:27
  59.6 3.8 %collective-permute-done = bf16[2,16,2048]{2,1,0:T(8,128)(2,1)S(1)} collective-permute-done((bf16[2,16,2048]{2,1,0:T(8,128)(2,1)S(1)}, bf16[2,16,2048]{2,1,0:T(8,128)(2,1)S(1)}, u32[]{:S(2)}, u32[]{:S(2)}) %collective-permute-start) | collective-permute-done | bytes 131104 | tf_op jit(solution)/shard_map/while/body/eval_jaxpr/ppermute | solution.py:10
  63.5 1.6 %fusion.53 = f32[2,16,1,2]{3,2,1,0:T(1,128)S(1)} fusion(bf16[2,16,2,2048]{3,2,1,0:T(2,128)(2,1)} %get-tuple-element.510, bf16[2,16,2048,1]{2,1,0,3:T(8,128)(2,1)S(1)} %bitcast.83), kind=kOutput, calls=%fused_computation.6.clone.1 | convolution fusion | flops 262144 | bytes 393472 | tf_op jit(solution)/shard_map/while/body/eval_jaxpr/mtkd,mtd->mtk/dot_general | solution.py:27
  69.0 3.8 %collective-permute-done = bf16[2,16,2048]{2,1,0:T(8,128)(2,1)S(1)} collective-permute-done((bf16[2,16,2048]{2,1,0:T(8,128)(2,1)S(1)}, bf16[2,16,2048]{2,1,0:T(8,128)(2,1)S(1)}, u32[]{:S(2)}, u32[]{:S(2)}) %collective-permute-start) | collective-permute-done | bytes 131104 | tf_op jit(solution)/shard_map/while/body/eval_jaxpr/ppermute | solution.py:10
  72.9 1.6 %fusion.53 = f32[2,16,1,2]{3,2,1,0:T(1,128)S(1)} fusion(bf16[2,16,2,2048]{3,2,1,0:T(2,128)(2,1)} %get-tuple-element.510, bf16[2,16,2048,1]{2,1,0,3:T(8,128)(2,1)S(1)} %bitcast.83), kind=kOutput, calls=%fused_computation.6.clone.1 | convolution fusion | flops 262144 | bytes 393472 | tf_op jit(solution)/shard_map/while/body/eval_jaxpr/mtkd,mtd->mtk/dot_general | solution.py:27
  78.3 4.6 %collective-permute-done = bf16[2,16,2048]{2,1,0:T(8,128)(2,1)S(1)} collective-permute-done((bf16[2,16,2048]{2,1,0:T(8,128)(2,1)S(1)}, bf16[2,16,2048]{2,1,0:T(8,128)(2,1)S(1)}, u32[]{:S(2)}, u32[]{:S(2)}) %collective-permute-start) | collective-permute-done | bytes 131104 | tf_op jit(solution)/shard_map/while/body/eval_jaxpr/ppermute | solution.py:10
  84.2 14.3 %all_gather.3 = bf16[2,32,2048]{2,1,0:T(8,128)(2,1)S(1)} all-gather(bf16[2,8,2048]{2,1,0:T(8,128)(2,1)S(1)} %convolution_convert_fusion.1), channel_id=1, replica_groups=mesh['section'=8,'expert'=4] {'expert'}, dimensions={1}, use_global_device_ids=true | all-gather | bytes 327680 | tf_op jit(solution)/shard_map/all_gather | solution.py:92
  98.4 6.1 %fusion.16 = bf16[64,1792]{1,0:T(8,128)(2,1)} fusion(bf16[64,2048]{1,0:T(8,128)(2,1)S(1)} %bitcast.85, bf16[1,1792,2048]{2,1,0:T(8,128)(2,1)} %param.15), kind=kOutput, calls=%fused_computation.24 | convolution fusion | flops 469876736 | bytes 7831552 | tf_op jit(solution)/shard_map/dot_general | solution.py:94
  104.5 5.1 %fusion.15 = bf16[1,1792,2048]{1,2,0:T(8,128)(2,1)} fusion(bf16[64,2048]{1,0:T(8,128)(2,1)S(1)} %bitcast.86, bf16[64,1792]{1,0:T(8,128)(2,1)S(1)} %bitcast.82), kind=kOutput, calls=%fused_computation.23 | convolution fusion | flops 473432064 | bytes 7831552 | tf_op jit(solution)/shard_map/dot_general | solution.py:98
  109.6 10.4 %copy.14 = bf16[1,1792,2048]{2,1,0:T(8,128)(2,1)} copy(bf16[1,1792,2048]{1,2,0:T(8,128)(2,1)} %fusion.15) | data formatting | bytes 14680064
  120.1 7.9 %all-reduce.2.cloned.1.call-done = f32[2048,8]{0,1:T(8,128)} async-done(((f32[2048,8]{0,1:T(8,128)}), f32[2048,8]{0,1:T(8,128)}) %all-reduce.2.cloned.1.call-update) | async-done | bytes 65552 | tf_op jit(solution)/shard_map/psum | solution.py:84
  128.0 1.5 %multiply_bitcast_fusion = f32[1,2048,8]{1,2,0:T(8,128)} fusion(f32[2048,8]{0,1:T(8,128)} %all-reduce.2.cloned.1.call-done), kind=kLoop, calls=%fused_computation.31 | loop fusion | flops 16384 | bytes 131072 | tf_op jit(solution)/shard_map/broadcast_in_dim | solution.py:106
  (74 shorter events, 32.6 us)
Async XLA Ops:
  7.2 97.4 %copy-start = (bf16[1,2,32,1792]{3,2,1,0:T(8,128)(2,1)S(1)}, bf16[1,2,32,1792]{3,2,1,0:T(8,128)(2,1)}, u32[]{:S(2)}) copy-start(bf16[1,2,32,1792]{3,2,1,0:T(8,128)(2,1)} %param.14) | copy-start | bytes 688132
  7.2 120.8 %all-reduce.2.cloned.1.call-start = ((), (), s32[]{:S(2)}) async-start(), calls=%async_computation | async-start | bytes 131072 | tf_op jit(solution)/shard_map/psum | solution.py:84
  9.5 74.1 %copy-start.3 = (s32[1,2,16,2]{2,3,1,0:T(2,128)S(1)}, s32[1,2,16,2]{2,3,1,0:T(2,128)}, u32[]{:S(2)}) copy-start(s32[1,2,16,2]{2,3,1,0:T(2,128)} %param.13) | copy-start | bytes 772
  12.6 3.2 %collective-permute-start = (bf16[2,16,2048]{2,1,0:T(8,128)(2,1)S(1)}, bf16[2,16,2048]{2,1,0:T(8,128)(2,1)S(1)}, u32[]{:S(2)}, u32[]{:S(2)}) collective-permute-start(bf16[2,16,2048]{2,1,0:T(8,128)(2,1)S(1)} %get-tuple-element.469), channel_id=1, source_target_pairs={{4,0},{8,4},{12,8},{16,12},{20,16},{24,20},{28,24},{5,1},{9,5},{13... | collective-permute-start | bytes 393224 | tf_op jit(solution)/shard_map/while/body/eval_jaxpr/ppermute | solution.py:10
  18.9 7.2 %collective-permute-start = (bf16[2,16,2048]{2,1,0:T(8,128)(2,1)S(1)}, bf16[2,16,2048]{2,1,0:T(8,128)(2,1)S(1)}, u32[]{:S(2)}, u32[]{:S(2)}) collective-permute-start(bf16[2,16,2048]{2,1,0:T(8,128)(2,1)S(1)} %get-tuple-element.469), channel_id=1, source_target_pairs={{4,0},{8,4},{12,8},{16,12},{20,16},{24,20},{28,24},{5,1},{9,5},{13... | collective-permute-start | bytes 393224 | tf_op jit(solution)/shard_map/while/body/eval_jaxpr/ppermute | solution.py:10
  29.1 6.3 %collective-permute-start = (bf16[2,16,2048]{2,1,0:T(8,128)(2,1)S(1)}, bf16[2,16,2048]{2,1,0:T(8,128)(2,1)S(1)}, u32[]{:S(2)}, u32[]{:S(2)}) collective-permute-start(bf16[2,16,2048]{2,1,0:T(8,128)(2,1)S(1)} %get-tuple-element.469), channel_id=1, source_target_pairs={{4,0},{8,4},{12,8},{16,12},{20,16},{24,20},{28,24},{5,1},{9,5},{13... | collective-permute-start | bytes 393224 | tf_op jit(solution)/shard_map/while/body/eval_jaxpr/ppermute | solution.py:10
  38.5 6.3 %collective-permute-start = (bf16[2,16,2048]{2,1,0:T(8,128)(2,1)S(1)}, bf16[2,16,2048]{2,1,0:T(8,128)(2,1)S(1)}, u32[]{:S(2)}, u32[]{:S(2)}) collective-permute-start(bf16[2,16,2048]{2,1,0:T(8,128)(2,1)S(1)} %get-tuple-element.469), channel_id=1, source_target_pairs={{4,0},{8,4},{12,8},{16,12},{20,16},{24,20},{28,24},{5,1},{9,5},{13... | collective-permute-start | bytes 393224 | tf_op jit(solution)/shard_map/while/body/eval_jaxpr/ppermute | solution.py:10
  47.8 6.3 %collective-permute-start = (bf16[2,16,2048]{2,1,0:T(8,128)(2,1)S(1)}, bf16[2,16,2048]{2,1,0:T(8,128)(2,1)S(1)}, u32[]{:S(2)}, u32[]{:S(2)}) collective-permute-start(bf16[2,16,2048]{2,1,0:T(8,128)(2,1)S(1)} %get-tuple-element.469), channel_id=1, source_target_pairs={{4,0},{8,4},{12,8},{16,12},{20,16},{24,20},{28,24},{5,1},{9,5},{13... | collective-permute-start | bytes 393224 | tf_op jit(solution)/shard_map/while/body/eval_jaxpr/ppermute | solution.py:10
  57.2 6.3 %collective-permute-start = (bf16[2,16,2048]{2,1,0:T(8,128)(2,1)S(1)}, bf16[2,16,2048]{2,1,0:T(8,128)(2,1)S(1)}, u32[]{:S(2)}, u32[]{:S(2)}) collective-permute-start(bf16[2,16,2048]{2,1,0:T(8,128)(2,1)S(1)} %get-tuple-element.469), channel_id=1, source_target_pairs={{4,0},{8,4},{12,8},{16,12},{20,16},{24,20},{28,24},{5,1},{9,5},{13... | collective-permute-start | bytes 393224 | tf_op jit(solution)/shard_map/while/body/eval_jaxpr/ppermute | solution.py:10
  66.5 6.3 %collective-permute-start = (bf16[2,16,2048]{2,1,0:T(8,128)(2,1)S(1)}, bf16[2,16,2048]{2,1,0:T(8,128)(2,1)S(1)}, u32[]{:S(2)}, u32[]{:S(2)}) collective-permute-start(bf16[2,16,2048]{2,1,0:T(8,128)(2,1)S(1)} %get-tuple-element.469), channel_id=1, source_target_pairs={{4,0},{8,4},{12,8},{16,12},{20,16},{24,20},{28,24},{5,1},{9,5},{13... | collective-permute-start | bytes 393224 | tf_op jit(solution)/shard_map/while/body/eval_jaxpr/ppermute | solution.py:10
  75.9 7.1 %collective-permute-start = (bf16[2,16,2048]{2,1,0:T(8,128)(2,1)S(1)}, bf16[2,16,2048]{2,1,0:T(8,128)(2,1)S(1)}, u32[]{:S(2)}, u32[]{:S(2)}) collective-permute-start(bf16[2,16,2048]{2,1,0:T(8,128)(2,1)S(1)} %get-tuple-element.469), channel_id=1, source_target_pairs={{4,0},{8,4},{12,8},{16,12},{20,16},{24,20},{28,24},{5,1},{9,5},{13... | collective-permute-start | bytes 393224 | tf_op jit(solution)/shard_map/while/body/eval_jaxpr/ppermute | solution.py:10
  82.9 0.6 copy-start.2
  82.9 26.7 %copy-start.1 = (bf16[2,16,2048]{2,1,0:T(8,128)(2,1)}, bf16[2,16,2048]{2,1,0:T(8,128)(2,1)S(1)}, u32[]{:S(2)}) copy-start(bf16[2,16,2048]{2,1,0:T(8,128)(2,1)S(1)} %get-tuple-element.304) | copy-start | bytes 393220
Sparse Core Ops, SparseCore 0:
  83.7 44.2 all-reduce.1
where the time goes:
time: 138 us; the launch traced here: 136 us
  matrix products  45.1 us (33%)
  waiting for transfers between devices  37.2 us (27%)
  blocking collectives  14.3 us (10%)
  between operations  14.2 us (10%)
  local copies, waits for them, and re-layouts  12.5 us (9%)
  starting transfers between devices  10.4 us (8%)
  other arithmetic  2.4 us (2%)
    ppermute x8, waiting for transfers between devices, passed_along(): return lax.ppermute(value, axis, pairs)  29.3 us
    all_gather x1, blocking collectives, per_device(): gathered = lax.all_gather(rows_out, 'expert', axis=1, tiled=True)  14.3 us
    dot_general x8, matrix products, backprop(): jnp.einsum('mtkd,mtd->mtk', outputs, cotangent, preferred_element_type=jn...  12.8 us
    unnamed x9, local copies, waits for them, and re-layouts  11.1 us
    ppermute x8, starting transfers between devices, passed_along(): return lax.ppermute(value, axis, pairs)  10.3 us
    dot_general x8, matrix products, backprop(): jnp.einsum('mte,de->mtd', logit_grad, weights, precision=lax.Precision.HI...  10.3 us
    dot_general x8, matrix products, backprop(): jnp.einsum('mtd,mte->de', inputs.astype(jnp.float32), logit_grad, precisi...  9.18 us
    psum x1, waiting for transfers between devices, per_device(): router_grad = lax.psum(router_acc, 'expert') / total_tokens  7.93 us
  transfers between devices with their start and end apart: 9, of which 9 were waited for; matrix products, arithmetic and copies ran while one was open for 23% of the time, Pallas kernels for 0%

commit v1 on v0

--- a/solution.py
+++ b/solution.py
@@ -89,7 +89,9 @@
     weight = down_w[0]
     ff_local = weight.shape[0]
     slot_total = saved_hidden.shape[1]
-    gathered = lax.all_gather(rows_out, "expert", axis=1, tiled=True)
+    gathered = jnp.concatenate(
+        lax.all_to_all(jnp.stack([rows_out] * lax.axis_size("expert")), "expert", 0, 0), axis=1
+    )
     flat_rows = gathered.reshape(-1, width)
     hidden_acc = lax.dot_general(
         flat_rows, weight, (((1,), (1,)), ((), ())), preferred_element_type=jnp.float32

time: 138 us -> 159 us (1.15)
  waiting for transfers between devices: 37.2 us -> 67.5 us
  blocking collectives: 14.3 us -> 0 us
  starting transfers between devices: 10.4 us -> 15.2 us
    psum x1, waiting for transfers between devices: 7.93 us -> 38.2 us  [per_device(): router_grad = lax.psum(router_acc, 'expert') / total_tokens]
    all_gather x1 -> x0, blocking collectives: 14.3 us -> none  [per_device(): gathered = lax.all_gather(rows_out, 'expert', axis=1, tiled=True)]
    all_to_all x0 -> x1, starting transfers between devices: none -> 4.87 us  [per_device(): lax.all_to_all(jnp.stack([rows_out] * lax.axis_size('expert')), 'expert',...]
  transfers between devices with their start and end apart: 9 -> 10, of which waited for: 9 -> 9; matrix products, arithmetic and copies ran while one was open for 23% -> 8% of each run, Pallas kernels for 0% -> 0%
where the time goes in v1:
time: 159 us; the launch traced here: 158 us
  waiting for transfers between devices  67.5 us (42%)
  matrix products  45.1 us (28%)
  starting transfers between devices  15.2 us (10%)
  between operations  14.2 us (9%)
  local copies, waits for them, and re-layouts  13.2 us (8%)
  other arithmetic  2.4 us (2%)
    psum x1, waiting for transfers between devices, per_device(): router_grad = lax.psum(router_acc, 'expert') / total_tokens  38.2 us
    ppermute x8, waiting for transfers between devices, passed_along(): return lax.ppermute(value, axis, pairs)  29.3 us
    dot_general x8, matrix products, backprop(): jnp.einsum('mtkd,mtd->mtk', outputs, cotangent, preferred_element_type=jn...  12.8 us
    unnamed x9, local copies, waits for them, and re-layouts  11.1 us
    ppermute x8, starting transfers between devices, passed_along(): return lax.ppermute(value, axis, pairs)  10.3 us
    dot_general x8, matrix products, backprop(): jnp.einsum('mte,de->mtd', logit_grad, weights, precision=lax.Precision.HI...  10.3 us
    dot_general x8, matrix products, backprop(): jnp.einsum('mtd,mte->de', inputs.astype(jnp.float32), logit_grad, precisi...  9.18 us
    dot_general x1, matrix products, per_device(): lax.dot_general(flat_rows, weight, (((1,), (1,)), ((), ())), preferred_el...  6.12 us
  transfers between devices with their start and end apart: 10, of which 9 were waited for; matrix products, arithmetic and copies ran while one was open for 8% of the time, Pallas kernels for 0%

profile of v1, /device:TPU:0, one launch (start us, length us, event | category | flops | bytes accessed | tf_op | source)
XLA Modules:
  0.0 157.9 jit_solution(12226914277627411776)
XLA Ops:
  8.0 1.5 fusion.22
  9.5 73.4 %while.22 = (s32[]{:T(128)}, bf16[2,16,2048]{2,1,0:T(8,128)(2,1)S(1)}, bf16[2,16,2048]{2,1,0:T(8,128)(2,1)S(1)}, bf16[2,16,2048]{2,1,0:T(8,128)(2,1)S(1)}, f32[2...) while((s32[]{:T(128)}, ...), condition=%wide.region_2.3_spmd.clone, body=%wide.region_1.2_spmd.clone.sunk | while | flops 13419140 | bytes 2428622 | solution.py:80
  9.7 1.6 %fusion.53 = f32[2,16,1,2]{3,2,1,0:T(1,128)S(1)} fusion(bf16[2,16,2,2048]{3,2,1,0:T(2,128)(2,1)} %get-tuple-element.518, bf16[2,16,2048,1]{2,1,0,3:T(8,128)(2,1)S(1)} %bitcast.85), kind=kOutput, calls=%fused_computation.6.clone.1 | convolution fusion | flops 262144 | bytes 393472 | tf_op jit(solution)/shard_map/while/body/eval_jaxpr/mtkd,mtd->mtk/dot_general | solution.py:27
  12.6 1.3 collective-permute-start
  15.9 1.6 %fusion.53 = f32[2,16,1,2]{3,2,1,0:T(1,128)S(1)} fusion(bf16[2,16,2,2048]{3,2,1,0:T(2,128)(2,1)} %get-tuple-element.518, bf16[2,16,2048,1]{2,1,0,3:T(8,128)(2,1)S(1)} %bitcast.85), kind=kOutput, calls=%fused_computation.6.clone.1 | convolution fusion | flops 262144 | bytes 393472 | tf_op jit(solution)/shard_map/while/body/eval_jaxpr/mtkd,mtd->mtk/dot_general | solution.py:27
  21.4 4.7 %collective-permute-done = bf16[2,16,2048]{2,1,0:T(8,128)(2,1)S(1)} collective-permute-done((bf16[2,16,2048]{2,1,0:T(8,128)(2,1)S(1)}, bf16[2,16,2048]{2,1,0:T(8,128)(2,1)S(1)}, u32[]{:S(2)}, u32[]{:S(2)}) %collective-permute-start) | collective-permute-done | bytes 131104 | tf_op jit(solution)/shard_map/while/body/eval_jaxpr/ppermute | solution.py:10
  26.1 1.6 %fusion.53 = f32[2,16,1,2]{3,2,1,0:T(1,128)S(1)} fusion(bf16[2,16,2,2048]{3,2,1,0:T(2,128)(2,1)} %get-tuple-element.518, bf16[2,16,2048,1]{2,1,0,3:T(8,128)(2,1)S(1)} %bitcast.85), kind=kOutput, calls=%fused_computation.6.clone.1 | convolution fusion | flops 262144 | bytes 393472 | tf_op jit(solution)/shard_map/while/body/eval_jaxpr/mtkd,mtd->mtk/dot_general | solution.py:27
  31.6 3.8 %collective-permute-done = bf16[2,16,2048]{2,1,0:T(8,128)(2,1)S(1)} collective-permute-done((bf16[2,16,2048]{2,1,0:T(8,128)(2,1)S(1)}, bf16[2,16,2048]{2,1,0:T(8,128)(2,1)S(1)}, u32[]{:S(2)}, u32[]{:S(2)}) %collective-permute-start) | collective-permute-done | bytes 131104 | tf_op jit(solution)/shard_map/while/body/eval_jaxpr/ppermute | solution.py:10
  35.5 1.6 %fusion.53 = f32[2,16,1,2]{3,2,1,0:T(1,128)S(1)} fusion(bf16[2,16,2,2048]{3,2,1,0:T(2,128)(2,1)} %get-tuple-element.518, bf16[2,16,2048,1]{2,1,0,3:T(8,128)(2,1)S(1)} %bitcast.85), kind=kOutput, calls=%fused_computation.6.clone.1 | convolution fusion | flops 262144 | bytes 393472 | tf_op jit(solution)/shard_map/while/body/eval_jaxpr/mtkd,mtd->mtk/dot_general | solution.py:27
  40.9 3.8 %collective-permute-done = bf16[2,16,2048]{2,1,0:T(8,128)(2,1)S(1)} collective-permute-done((bf16[2,16,2048]{2,1,0:T(8,128)(2,1)S(1)}, bf16[2,16,2048]{2,1,0:T(8,128)(2,1)S(1)}, u32[]{:S(2)}, u32[]{:S(2)}) %collective-permute-start) | collective-permute-done | bytes 131104 | tf_op jit(solution)/shard_map/while/body/eval_jaxpr/ppermute | solution.py:10
  44.8 1.6 %fusion.53 = f32[2,16,1,2]{3,2,1,0:T(1,128)S(1)} fusion(bf16[2,16,2,2048]{3,2,1,0:T(2,128)(2,1)} %get-tuple-element.518, bf16[2,16,2048,1]{2,1,0,3:T(8,128)(2,1)S(1)} %bitcast.85), kind=kOutput, calls=%fused_computation.6.clone.1 | convolution fusion | flops 262144 | bytes 393472 | tf_op jit(solution)/shard_map/while/body/eval_jaxpr/mtkd,mtd->mtk/dot_general | solution.py:27
  50.3 3.8 %collective-permute-done = bf16[2,16,2048]{2,1,0:T(8,128)(2,1)S(1)} collective-permute-done((bf16[2,16,2048]{2,1,0:T(8,128)(2,1)S(1)}, bf16[2,16,2048]{2,1,0:T(8,128)(2,1)S(1)}, u32[]{:S(2)}, u32[]{:S(2)}) %collective-permute-start) | collective-permute-done | bytes 131104 | tf_op jit(solution)/shard_map/while/body/eval_jaxpr/ppermute | solution.py:10
  54.2 1.6 %fusion.53 = f32[2,16,1,2]{3,2,1,0:T(1,128)S(1)} fusion(bf16[2,16,2,2048]{3,2,1,0:T(2,128)(2,1)} %get-tuple-element.518, bf16[2,16,2048,1]{2,1,0,3:T(8,128)(2,1)S(1)} %bitcast.85), kind=kOutput, calls=%fused_computation.6.clone.1 | convolution fusion | flops 262144 | bytes 393472 | tf_op jit(solution)/shard_map/while/body/eval_jaxpr/mtkd,mtd->mtk/dot_general | solution.py:27
  59.6 3.8 %collective-permute-done = bf16[2,16,2048]{2,1,0:T(8,128)(2,1)S(1)} collective-permute-done((bf16[2,16,2048]{2,1,0:T(8,128)(2,1)S(1)}, bf16[2,16,2048]{2,1,0:T(8,128)(2,1)S(1)}, u32[]{:S(2)}, u32[]{:S(2)}) %collective-permute-start) | collective-permute-done | bytes 131104 | tf_op jit(solution)/shard_map/while/body/eval_jaxpr/ppermute | solution.py:10
  63.5 1.6 %fusion.53 = f32[2,16,1,2]{3,2,1,0:T(1,128)S(1)} fusion(bf16[2,16,2,2048]{3,2,1,0:T(2,128)(2,1)} %get-tuple-element.518, bf16[2,16,2048,1]{2,1,0,3:T(8,128)(2,1)S(1)} %bitcast.85), kind=kOutput, calls=%fused_computation.6.clone.1 | convolution fusion | flops 262144 | bytes 393472 | tf_op jit(solution)/shard_map/while/body/eval_jaxpr/mtkd,mtd->mtk/dot_general | solution.py:27
  69.0 3.8 %collective-permute-done = bf16[2,16,2048]{2,1,0:T(8,128)(2,1)S(1)} collective-permute-done((bf16[2,16,2048]{2,1,0:T(8,128)(2,1)S(1)}, bf16[2,16,2048]{2,1,0:T(8,128)(2,1)S(1)}, u32[]{:S(2)}, u32[]{:S(2)}) %collective-permute-start) | collective-permute-done | bytes 131104 | tf_op jit(solution)/shard_map/while/body/eval_jaxpr/ppermute | solution.py:10
  72.9 1.6 %fusion.53 = f32[2,16,1,2]{3,2,1,0:T(1,128)S(1)} fusion(bf16[2,16,2,2048]{3,2,1,0:T(2,128)(2,1)} %get-tuple-element.518, bf16[2,16,2048,1]{2,1,0,3:T(8,128)(2,1)S(1)} %bitcast.85), kind=kOutput, calls=%fused_computation.6.clone.1 | convolution fusion | flops 262144 | bytes 393472 | tf_op jit(solution)/shard_map/while/body/eval_jaxpr/mtkd,mtd->mtk/dot_general | solution.py:27
  78.3 4.6 %collective-permute-done = bf16[2,16,2048]{2,1,0:T(8,128)(2,1)S(1)} collective-permute-done((bf16[2,16,2048]{2,1,0:T(8,128)(2,1)S(1)}, bf16[2,16,2048]{2,1,0:T(8,128)(2,1)S(1)}, u32[]{:S(2)}, u32[]{:S(2)}) %collective-permute-start) | collective-permute-done | bytes 131104 | tf_op jit(solution)/shard_map/while/body/eval_jaxpr/ppermute | solution.py:10
  84.9 4.9 %all-to-all-start = ((bf16[4,2,8,2048]{3,2,1,0:T(8,128)(2,1)}), bf16[4,2,8,2048]{3,2,1,0:T(8,128)(2,1)S(1)}, u32[]{:S(2)}, u32[]{:S(2)}) async-start(bf16[4,2,8,2048]{3,2,1,0:T(8,128)(2,1)} %stack.3), calls=%async_computation | async-start | bytes 524288 | tf_op jit(solution)/shard_map/all_to_all | solution.py:93
  89.7 38.2 %all-reduce.2.cloned.1.call-done = f32[2048,8]{0,1:T(8,128)} async-done(((f32[2048,8]{0,1:T(8,128)}), f32[2048,8]{0,1:T(8,128)}) %all-reduce.2.cloned.1.call-update) | async-done | bytes 65552 | tf_op jit(solution)/shard_map/psum | solution.py:84
  127.9 1.5 multiply_bitcast_fusion
  129.4 6.1 %fusion.16 = bf16[64,1792]{1,0:T(8,128)(2,1)} fusion(bf16[64,2048]{1,0:T(8,128)(2,1)S(1)} %bitcast.87, bf16[1,1792,2048]{2,1,0:T(8,128)(2,1)} %param.15), kind=kOutput, calls=%fused_computation.24 | convolution fusion | flops 469876736 | bytes 7831552 | tf_op jit(solution)/shard_map/dot_general | solution.py:96
  135.5 5.1 %fusion.15 = bf16[1,1792,2048]{1,2,0:T(8,128)(2,1)} fusion(bf16[64,2048]{1,0:T(8,128)(2,1)S(1)} %bitcast.88, bf16[64,1792]{1,0:T(8,128)(2,1)S(1)} %bitcast.84), kind=kOutput, calls=%fused_computation.23 | convolution fusion | flops 473432064 | bytes 7831552 | tf_op jit(solution)/shard_map/dot_general | solution.py:100
  140.6 10.4 %copy.23 = bf16[1,1792,2048]{2,1,0:T(8,128)(2,1)} copy(bf16[1,1792,2048]{1,2,0:T(8,128)(2,1)} %fusion.15) | data formatting | bytes 14680064
  (77 shorter events, 33.4 us)
Async XLA Ops:
  7.2 128.4 %copy-start = (bf16[1,2,32,1792]{3,2,1,0:T(8,128)(2,1)S(1)}, bf16[1,2,32,1792]{3,2,1,0:T(8,128)(2,1)}, u32[]{:S(2)}) copy-start(bf16[1,2,32,1792]{3,2,1,0:T(8,128)(2,1)} %param.14) | copy-start | bytes 688132
  7.2 120.7 %all-reduce.2.cloned.1.call-start = ((), (), s32[]{:S(2)}) async-start(), calls=%async_computation.1 | async-start | bytes 131072 | tf_op jit(solution)/shard_map/psum | solution.py:84
  9.5 74.1 %copy-start.3 = (s32[1,2,16,2]{2,3,1,0:T(2,128)S(1)}, s32[1,2,16,2]{2,3,1,0:T(2,128)}, u32[]{:S(2)}) copy-start(s32[1,2,16,2]{2,3,1,0:T(2,128)} %param.13) | copy-start | bytes 772
  12.6 3.2 %collective-permute-start = (bf16[2,16,2048]{2,1,0:T(8,128)(2,1)S(1)}, bf16[2,16,2048]{2,1,0:T(8,128)(2,1)S(1)}, u32[]{:S(2)}, u32[]{:S(2)}) collective-permute-start(bf16[2,16,2048]{2,1,0:T(8,128)(2,1)S(1)} %get-tuple-element.477), channel_id=1, source_target_pairs={{4,0},{8,4},{12,8},{16,12},{20,16},{24,20},{28,24},{5,1},{9,5},{13... | collective-permute-start | bytes 393224 | tf_op jit(solution)/shard_map/while/body/eval_jaxpr/ppermute | solution.py:10
  18.9 7.2 %collective-permute-start = (bf16[2,16,2048]{2,1,0:T(8,128)(2,1)S(1)}, bf16[2,16,2048]{2,1,0:T(8,128)(2,1)S(1)}, u32[]{:S(2)}, u32[]{:S(2)}) collective-permute-start(bf16[2,16,2048]{2,1,0:T(8,128)(2,1)S(1)} %get-tuple-element.477), channel_id=1, source_target_pairs={{4,0},{8,4},{12,8},{16,12},{20,16},{24,20},{28,24},{5,1},{9,5},{13... | collective-permute-start | bytes 393224 | tf_op jit(solution)/shard_map/while/body/eval_jaxpr/ppermute | solution.py:10
  29.1 6.3 %collective-permute-start = (bf16[2,16,2048]{2,1,0:T(8,128)(2,1)S(1)}, bf16[2,16,2048]{2,1,0:T(8,128)(2,1)S(1)}, u32[]{:S(2)}, u32[]{:S(2)}) collective-permute-start(bf16[2,16,2048]{2,1,0:T(8,128)(2,1)S(1)} %get-tuple-element.477), channel_id=1, source_target_pairs={{4,0},{8,4},{12,8},{16,12},{20,16},{24,20},{28,24},{5,1},{9,5},{13... | collective-permute-start | bytes 393224 | tf_op jit(solution)/shard_map/while/body/eval_jaxpr/ppermute | solution.py:10
  38.5 6.3 %collective-permute-start = (bf16[2,16,2048]{2,1,0:T(8,128)(2,1)S(1)}, bf16[2,16,2048]{2,1,0:T(8,128)(2,1)S(1)}, u32[]{:S(2)}, u32[]{:S(2)}) collective-permute-start(bf16[2,16,2048]{2,1,0:T(8,128)(2,1)S(1)} %get-tuple-element.477), channel_id=1, source_target_pairs={{4,0},{8,4},{12,8},{16,12},{20,16},{24,20},{28,24},{5,1},{9,5},{13... | collective-permute-start | bytes 393224 | tf_op jit(solution)/shard_map/while/body/eval_jaxpr/ppermute | solution.py:10
  47.8 6.3 %collective-permute-start = (bf16[2,16,2048]{2,1,0:T(8,128)(2,1)S(1)}, bf16[2,16,2048]{2,1,0:T(8,128)(2,1)S(1)}, u32[]{:S(2)}, u32[]{:S(2)}) collective-permute-start(bf16[2,16,2048]{2,1,0:T(8,128)(2,1)S(1)} %get-tuple-element.477), channel_id=1, source_target_pairs={{4,0},{8,4},{12,8},{16,12},{20,16},{24,20},{28,24},{5,1},{9,5},{13... | collective-permute-start | bytes 393224 | tf_op jit(solution)/shard_map/while/body/eval_jaxpr/ppermute | solution.py:10
  57.2 6.3 %collective-permute-start = (bf16[2,16,2048]{2,1,0:T(8,128)(2,1)S(1)}, bf16[2,16,2048]{2,1,0:T(8,128)(2,1)S(1)}, u32[]{:S(2)}, u32[]{:S(2)}) collective-permute-start(bf16[2,16,2048]{2,1,0:T(8,128)(2,1)S(1)} %get-tuple-element.477), channel_id=1, source_target_pairs={{4,0},{8,4},{12,8},{16,12},{20,16},{24,20},{28,24},{5,1},{9,5},{13... | collective-permute-start | bytes 393224 | tf_op jit(solution)/shard_map/while/body/eval_jaxpr/ppermute | solution.py:10
  66.5 6.3 %collective-permute-start = (bf16[2,16,2048]{2,1,0:T(8,128)(2,1)S(1)}, bf16[2,16,2048]{2,1,0:T(8,128)(2,1)S(1)}, u32[]{:S(2)}, u32[]{:S(2)}) collective-permute-start(bf16[2,16,2048]{2,1,0:T(8,128)(2,1)S(1)} %get-tuple-element.477), channel_id=1, source_target_pairs={{4,0},{8,4},{12,8},{16,12},{20,16},{24,20},{28,24},{5,1},{9,5},{13... | collective-permute-start | bytes 393224 | tf_op jit(solution)/shard_map/while/body/eval_jaxpr/ppermute | solution.py:10
  75.9 7.1 %collective-permute-start = (bf16[2,16,2048]{2,1,0:T(8,128)(2,1)S(1)}, bf16[2,16,2048]{2,1,0:T(8,128)(2,1)S(1)}, u32[]{:S(2)}, u32[]{:S(2)}) collective-permute-start(bf16[2,16,2048]{2,1,0:T(8,128)(2,1)S(1)} %get-tuple-element.477), channel_id=1, source_target_pairs={{4,0},{8,4},{12,8},{16,12},{20,16},{24,20},{28,24},{5,1},{9,5},{13... | collective-permute-start | bytes 393224 | tf_op jit(solution)/shard_map/while/body/eval_jaxpr/ppermute | solution.py:10
  82.9 0.6 copy-start.2
  82.9 57.6 %copy-start.1 = (bf16[2,16,2048]{2,1,0:T(8,128)(2,1)}, bf16[2,16,2048]{2,1,0:T(8,128)(2,1)S(1)}, u32[]{:S(2)}) copy-start(bf16[2,16,2048]{2,1,0:T(8,128)(2,1)S(1)} %get-tuple-element.304) | copy-start | bytes 393220
  84.9 44.5 %all-to-all-start = ((bf16[4,2,8,2048]{3,2,1,0:T(8,128)(2,1)}), bf16[4,2,8,2048]{3,2,1,0:T(8,128)(2,1)S(1)}, u32[]{:S(2)}, u32[]{:S(2)}) async-start(bf16[4,2,8,2048]{3,2,1,0:T(8,128)(2,1)} %stack.3), calls=%async_computation | async-start | bytes 524288 | tf_op jit(solution)/shard_map/all_to_all | solution.py:93
Sparse Core Ops, SparseCore 0:
  83.7 44.1 all-reduce.1
